TPU v7x, 8 devices: a whole 2x2x1 slice. The times are simulated.
8 devices in a mesh: inst: 1 (over z), qy: 2 (over y), qx: 4 (over x, core).
Axes of the slice: x: 2, y: 2, z: 1, core: 2. Of those that a mesh axis runs over, the one named last changes fastest.
Arguments:
- cost_diag: float32 [32768], P(('inst', 'qx', 'qy'))
- gamma_angles: float32 [4], replicated
- beta_angles: float32 [4], replicated
Outputs:
- output 1: float32 [1], P('inst')
- output 2: float32 [32768], P(('inst', 'qx', 'qy'))
- output 3: float32 [32768], P(('inst', 'qx', 'qy'))
All inputs are finite; a program needn't handle non-finite values.
Results may differ from a plain program's by a relative error of at most 0.001.
Values sent between devices are 32-bit elements.
A program may use at most 1 GiB of HBM per device.

v0:
```python
import functools
import math

import jax
import jax.numpy as jnp
from jax import lax
from jax.experimental import pallas as pl
from jax.experimental.pallas import tpu as pltpu
from jax.sharding import PartitionSpec as P

MESH = pl.DeviceIdType.MESH
ROWS, LANES = 32, 128
F32 = jnp.float32


def gather_kernel(cost_ref, all_ref, local_sem, send_sem, recv_sem):
    qx, qy = lax.axis_index('qx'), lax.axis_index('qy')
    other_y = 1 - qy
    other_c = qx + 1 - 2 * lax.rem(qx, 2)
    peers = [{'qx': qx, 'qy': other_y}, {'qx': other_c, 'qy': qy}, {'qx': other_c, 'qy': other_y}]
    barrier = pltpu.get_barrier_semaphore()
    for peer in peers:
        pl.semaphore_signal(barrier, inc=1, device_id=peer, device_id_type=MESH)
    local = pltpu.make_async_copy(cost_ref, all_ref.at[0], local_sem)
    local.start()
    pl.semaphore_wait(barrier, 3)
    local.wait()
    copies = []
    for k, peer in enumerate(peers):
        copies.append(pltpu.make_async_remote_copy(
            src_ref=all_ref.at[0], dst_ref=all_ref.at[k + 1],
            send_sem=send_sem.at[k], recv_sem=recv_sem.at[k],
            device_id=peer, device_id_type=MESH))
    for copy in copies:
        copy.start()
    for copy in copies:
        copy.wait()


INV_2PI = 0.15915494309189535
P1, P2, P3 = 6.28125, 1.9350051879882812e-3, 3.0199159819568e-7


def sincos(x):
    n = jnp.round(x * INV_2PI)
    t = (((x - n * P1) - n * P2) - n * P3) * 0.25
    z = t * t
    s = ((-1.9515295891e-4 * z + 8.3321608736e-3) * z - 1.6666654611e-1) * z * t + t
    c = ((2.443315711809948e-5 * z - 1.388731625493765e-3) * z + 4.166664568298827e-2) * (z * z) + (1.0 - 0.5 * z)
    for _ in range(2):
        d = s + s
        c, s = 1.0 - d * s, d * c
    return c, s


def flip(x, mask):
    idx = lax.broadcasted_iota(jnp.int32, x.shape, 0) ^ mask
    return jnp.take_along_axis(x, idx, axis=0)


def pair_mix(re, im, i, j, cb, sb):
    re, im = list(re), list(im)
    for v in range(len(re)):
        if v & (1 << i) or v & (1 << j):
            continue
        a, b, c, d = v, v | 1 << i, v | 1 << j, v | 1 << i | 1 << j
        pr, pi = re[a] + re[d], im[a] + im[d]
        mr, mi = re[a] - re[d], im[a] - im[d]
        qr, qi = re[b] + re[c], im[b] + im[c]
        nr, ni = re[b] - re[c], im[b] - im[c]
        ur, ui = cb * pr + sb * qi, cb * pi - sb * qr
        vr, vi = cb * qr + sb * pi, cb * qi - sb * pr
        re[a], im[a], re[d], im[d] = ur + mr, ui + mi, ur - mr, ui - mi
        re[b], im[b], re[c], im[c] = vr + nr, vi + ni, vr - nr, vi - ni
    return re, im


def sublane_mix(re, im, c, s, cb, sb):
    out_re, out_im = [], []
    for r, i in zip(re, im):
        fr, fi = flip(r, 3), flip(i, 3)
        pr, pi, mr, mi = r + fr, i + fi, r - fr, i - fi
        qr, qi = flip(pr, 1), flip(pi, 1)
        r, i = (cb * pr + mr) + sb * qi, (cb * pi + mi) - sb * qr
        fr, fi = flip(r, 4), flip(i, 4)
        out_re.append(c * r + s * fi)
        out_im.append(c * i - s * fr)
    return out_re, out_im


def row_mix(re, im, c, s, cb, sb):
    re, im = pair_mix(re, im, 0, 1, cb, sb)
    re, im = pair_mix(re, im, 2, 3, cb, sb)
    return sublane_mix(re, im, 0.125 * c, 0.125 * s, cb, sb)


def transpose(blocks):
    whole = jnp.transpose(jnp.concatenate(blocks, axis=0))
    return [whole[8 * v:8 * v + 8] for v in range(16)]


def reverse_rows(blocks):
    return [flip(blocks[15 - v], 7) for v in range(16)]


def circuit_kernel(layers, amp0, cost_ref, gamma_ref, beta_ref, energy_ref, re_ref, im_ref):
    cost = [cost_ref[v // 4, 8 * (v % 4):8 * (v % 4) + 8, :] for v in range(16)]
    cost_t = transpose(cost)
    re = im = None
    for layer in range(layers):
        now = cost if layer % 2 == 0 else cost_t
        gamma = gamma_ref[layer]
        phases = [sincos(gamma * x) for x in now]
        if layer == 0:
            re, im = [amp0 * c for c, _ in phases], [-amp0 * s for _, s in phases]
        else:
            re, im = ([r * c + i * s for r, i, (c, s) in zip(re, im, phases)],
                      [i * c - r * s for r, i, (c, s) in zip(re, im, phases)])
        beta = jnp.full((8, LANES), beta_ref[layer], F32)
        c, s, cb, sb = jnp.cos(0.5 * beta), jnp.sin(0.5 * beta), jnp.cos(beta), jnp.sin(beta)
        re, im = row_mix(re, im, c, s, cb, sb)
        back_re, back_im = reverse_rows(re), reverse_rows(im)
        re, im = transpose(re), transpose(im)
        back_re, back_im = reverse_rows(transpose(back_re)), reverse_rows(transpose(back_im))
        re, im = ([c * r + s * b for r, b in zip(re, back_im)],
                  [c * i - s * b for i, b in zip(im, back_re)])
        re, im = row_mix(re, im, c, s, cb, sb)
    now = cost if layers % 2 == 0 else cost_t
    if layers % 2:
        re_n, im_n = transpose(re), transpose(im)
    else:
        re_n, im_n = re, im
    for v in range(4):
        re_ref[8 * v:8 * v + 8, :] = re_n[v]
        im_ref[8 * v:8 * v + 8, :] = im_n[v]
    terms = [x * (r * r + i * i) for x, r, i in zip(now, re, im)]
    while len(terms) > 1:
        terms = [a + b for a, b in zip(terms[::2], terms[1::2])]
    energy_ref[0] = 2.0 * jnp.sum(terms[0])


def solution(mesh):
    spec = P(('inst', 'qx', 'qy'))

    def device_body(cost, gamma, beta):
        layers = gamma.shape[0]
        vmem = pl.BlockSpec(memory_space=pltpu.VMEM)
        smem = pl.BlockSpec(memory_space=pltpu.SMEM)
        gathered = pl.pallas_call(
            gather_kernel,
            out_shape=jax.ShapeDtypeStruct((4, ROWS, LANES), F32),
            in_specs=[pl.BlockSpec(memory_space=pl.ANY)],
            out_specs=vmem,
            scratch_shapes=[pltpu.SemaphoreType.DMA, pltpu.SemaphoreType.DMA((3,)), pltpu.SemaphoreType.DMA((3,))],
            compiler_params=pltpu.CompilerParams(collective_id=0, has_side_effects=True),
            name='gather')(cost.reshape(ROWS, LANES))
        amp0 = 2.0 ** (-7.5)
        energy, re, im = pl.pallas_call(
            functools.partial(circuit_kernel, layers, amp0),
            out_shape=[jax.ShapeDtypeStruct((1,), F32)] + [jax.ShapeDtypeStruct((ROWS, LANES), F32)] * 2,
            in_specs=[vmem, smem, smem],
            out_specs=[smem, vmem, vmem],
            name='circuit')(gathered, gamma, beta)
        return energy, re.reshape(-1), im.reshape(-1)

    return jax.shard_map(device_body, mesh=mesh, in_specs=(spec, P(), P()), out_specs=(P('inst'), spec, spec), check_vma=False)
```

profile of v0, /device:TPU:0, one launch (start us, length us, event | category | flops | bytes accessed | tf_op | source)
XLA Modules:
  0.0 10.1 jit_solution(16107585141355759096)
XLA Ops:
  0.6 6.5 %gather.1.cost_ref = f32[4,32,128]{2,1,0:T(8,128)} custom-call(f32[32,128]{1,0:T(8,128)} %bitcast.3), custom_call_target="tpu_custom_call" | custom-call | tf_op jit(solution)/shard_map/gather/pallas_call | solution.py:149
  7.1 3.0 %circuit.1 = (f32[1]{0:T(128)}, f32[32,128]{1,0:T(8,128)}, f32[32,128]{1,0:T(8,128)}) custom-call(f32[4,32,128]{2,1,0:T(8,128)} %gather.1.cost_ref, f32[4]{0:T(128)} %gamma_ref.1, f32[4]{0:T(128)} %beta_ref.1), custom_call_target="tpu_custom_call" | custom-call | tf_op jit(solution)/shard_map/circuit/pallas_call | solution.py:158
where the time goes:
time: 10.3 us; the launch traced here: 10.1 us
  Pallas kernels  9.46 us (92%)
  between operations  0.64 us (6%)
    pallas_call x1, Pallas kernels, device_body(): pl.pallas_call(gather_kernel, out_shape=jax.ShapeDtypeStruct((4, ROWS, LA...  6.51 us
    pallas_call x1, Pallas kernels, device_body(): pl.pallas_call(functools.partial(circuit_kernel, layers, amp0), out_shape...  2.95 us

commit v1 on v0

--- a/solution.py
+++ b/solution.py
@@ -149,10 +149,10 @@
         gathered = pl.pallas_call(
             gather_kernel,
             out_shape=jax.ShapeDtypeStruct((4, ROWS, LANES), F32),
-            in_specs=[pl.BlockSpec(memory_space=pl.ANY)],
+            in_specs=[pl.BlockSpec(memory_space=pltpu.HBM)],
             out_specs=vmem,
             scratch_shapes=[pltpu.SemaphoreType.DMA, pltpu.SemaphoreType.DMA((3,)), pltpu.SemaphoreType.DMA((3,))],
-            compiler_params=pltpu.CompilerParams(collective_id=0, has_side_effects=True),
+            compiler_params=pltpu.CompilerParams(collective_id=0, has_side_effects=True, vmem_limit_bytes=2 << 20),
             name='gather')(cost.reshape(ROWS, LANES))
         amp0 = 2.0 ** (-7.5)
         energy, re, im = pl.pallas_call(
@@ -160,6 +160,7 @@
             out_shape=[jax.ShapeDtypeStruct((1,), F32)] + [jax.ShapeDtypeStruct((ROWS, LANES), F32)] * 2,
             in_specs=[vmem, smem, smem],
             out_specs=[smem, vmem, vmem],
+            compiler_params=pltpu.CompilerParams(vmem_limit_bytes=4 << 20),
             name='circuit')(gathered, gamma, beta)
         return energy, re.reshape(-1), im.reshape(-1)
 

time: 10.3 us -> 9.54 us (0.926)
  Pallas kernels: 9.46 us -> 7.97 us
  local copies, waits for them, and re-layouts: 0 us -> 0.72 us
    pallas_call x1, Pallas kernels: 6.51 us -> 5.32 us  [device_body(): pl.pallas_call(gather_kernel, out_shape=jax.ShapeDtypeStruct((4, ROWS, LA...]
    unnamed x0 -> x6, local copies, waits for them, and re-layouts: none -> 0.72 us
    pallas_call x1, Pallas kernels: 2.95 us -> 2.64 us  [device_body(): pl.pallas_call(functools.partial(circuit_kernel, layers, amp0), out_shape...]
where the time goes in v1:
time: 9.54 us; the launch traced here: 9.35 us
  Pallas kernels  7.97 us (84%)
  local copies, waits for them, and re-layouts  0.72 us (8%)
  between operations  0.66 us (7%)
    pallas_call x1, Pallas kernels, device_body(): pl.pallas_call(gather_kernel, out_shape=jax.ShapeDtypeStruct((4, ROWS, LA...  5.32 us
    pallas_call x1, Pallas kernels, device_body(): pl.pallas_call(functools.partial(circuit_kernel, layers, amp0), out_shape...  2.64 us
    unnamed x6, local copies, waits for them, and re-layouts  0.72 us

profile of v1, /device:TPU:0, one launch (start us, length us, event | category | flops | bytes accessed | tf_op | source)
XLA Modules:
  0.0 9.3 jit_solution(17013421482791574580)
XLA Ops:
  0.6 0.0 copy-start
  0.6 0.7 %copy-done = f32[4096]{0:T(1024)S(1)} copy-done((f32[4096]{0:T(1024)S(1)}, f32[4096]{0:T(1024)}, u32[]{:S(2)}) %copy-start) | copy-done | bytes 16408
  1.3 0.0 copy-start.1
  1.4 0.0 copy-start.2
  1.4 5.3 %gather.1.cost_ref = f32[4,32,128]{2,1,0:T(8,128)S(1)} custom-call(f32[32,128]{1,0:T(8,128)S(1)} %bitcast.3), custom_call_target="tpu_custom_call" | custom-call | tf_op jit(solution)/shard_map/gather/pallas_call | solution.py:149
  6.7 0.0 copy-done.1
  6.7 0.0 copy-done.2
  6.7 2.6 %circuit.1 = (f32[1]{0:T(128)}, f32[32,128]{1,0:T(8,128)}, f32[32,128]{1,0:T(8,128)}) custom-call(f32[4,32,128]{2,1,0:T(8,128)S(1)} %gather.1.cost_ref, f32[4]{0:T(128)S(1)} %copy-done.1, f32[4]{0:T(128)S(1)} %copy-done.2), custom_call_target="tpu_custom_call" | custom-call | tf_op jit(solution)/shard_map/circuit/pallas_call | solution.py:158
Async XLA Ops:
  0.6 0.7 %copy-start = (f32[4096]{0:T(1024)S(1)}, f32[4096]{0:T(1024)}, u32[]{:S(2)}) copy-start(f32[4096]{0:T(1024)} %param.3) | copy-start | bytes 49156
  1.3 5.3 %copy-start.1 = (f32[4]{0:T(128)S(1)}, f32[4]{0:T(128)}, u32[]{:S(2)}) copy-start(f32[4]{0:T(128)} %gamma_ref.1) | copy-start | bytes 52
  1.4 5.3 %copy-start.2 = (f32[4]{0:T(128)S(1)}, f32[4]{0:T(128)}, u32[]{:S(2)}) copy-start(f32[4]{0:T(128)} %beta_ref.1) | copy-start | bytes 52
